TPU v7x, 32 devices: a whole 2x2x4 slice. The times are simulated.
32 devices in a mesh: seq: 2 (over core), row: 4 (over z), col: 4 (over y, x).
Axes of the slice: x: 2, y: 2, z: 4, core: 2. Of those that a mesh axis runs over, the one named last changes fastest.
Arguments:
- alignment: bfloat16 [128, 32, 256], P('seq', ('row', 'col')), may hold values from -6 to 6, as said below
- row_mask: int32 [128, 32], P('seq', ('row', 'col')), may hold values 0 or 1
- norm_gain: float32 [256], replicated, may hold values from 0.5 to 1.5
- norm_bias: float32 [256], replicated, may hold values from -1.5 to 1.5
- left_weight: bfloat16 [256, 32], replicated, may hold values from -0.375 to 0.375
- left_bias: float32 [32], replicated, may hold values from -6 to 6
- right_weight: bfloat16 [256, 32], replicated, may hold values from -0.375 to 0.375
- right_bias: float32 [32], replicated, may hold values from -6 to 6
- pair_weight: float32 [1024, 128], replicated, may hold values from -0.375 to 0.375
- pair_state: bfloat16 [32, 32, 128], P('row', 'col'), may hold values from -6 to 6
Outputs:
- new_pair: bfloat16 [32, 32, 128], P('row', 'col')
Inputs may be any that keep to these rules, and one draw needn't show every extreme that they name: alignment rows come in 8 clusters of consecutive rows that share a profile per residue, entries within -6 to 6.
All inputs are finite; a program needn't handle non-finite values.
Results may differ from a plain program's by a relative error of at most 0.001.
Values may be sent and summed in bfloat16 or wider, within the bound.
A program may use at most 64 MiB of HBM per device.

v0:
```python
import jax
import jax.numpy as jnp
from jax import lax
from jax.sharding import PartitionSpec as P

variance_floor = 1e-05
count_floor = 0.001


def layer_norm(alignment, norm_gain, norm_bias):
    values = alignment.astype(jnp.float32)
    center = jnp.mean(values, axis=-1, keepdims=True)
    spread = jnp.mean((values - center) ** 2, axis=-1, keepdims=True)
    return ((values - center) * lax.rsqrt(spread + variance_floor) * norm_gain + norm_bias).astype(
        jnp.bfloat16
    )


def project(normed, weight, offset, mask_float, marker):
    result = (
        (jnp.dot(normed, weight, preferred_element_type=jnp.float32) + offset)
        * mask_float[:, :, None]
    ).astype(jnp.bfloat16)
    return jnp.concatenate([result, marker], axis=-1)


def outer_block(left_part, right_part):
    depth, left_count, width = left_part.shape
    right_count = right_part.shape[1]
    product = lax.dot_general(
        left_part.reshape(depth, left_count * width),
        right_part.reshape(depth, right_count * width),
        (((0,), (0,)), ((), ())),
        preferred_element_type=jnp.float32,
    )
    return product.reshape(left_count, width, right_count, width).transpose(0, 2, 1, 3)


def split_joint(joint):
    channels = joint.shape[-1] - 1
    flat_sums = joint[:, :, :channels, :channels].reshape(
        joint.shape[0], joint.shape[1], channels * channels
    )
    count_sums = joint[:, :, channels, channels]
    return (flat_sums, count_sums)


def finish(flat_sums, count_sums, pair_rows, pair_weight):
    update = (
        jnp.dot(flat_sums, pair_weight, precision=lax.Precision.HIGHEST)
        / (count_floor + count_sums)[:, :, None]
    )
    return (pair_rows.astype(jnp.float32) + update).astype(jnp.bfloat16)


def column_block(whole_right):
    block_width = whole_right.shape[1] // lax.axis_size("col")
    return lax.dynamic_slice_in_dim(
        whole_right, lax.axis_index("col") * block_width, block_width, 1
    )


def on_device(
    alignment,
    row_mask,
    norm_gain,
    norm_bias,
    left_weight,
    left_bias,
    right_weight,
    right_bias,
    pair_weight,
    pair_state,
):
    normed = layer_norm(alignment, norm_gain, norm_bias)
    mask_float = row_mask.astype(jnp.float32)
    marker = mask_float.astype(jnp.bfloat16)[:, :, None]
    left = project(normed, left_weight, left_bias, mask_float, marker)
    right = project(normed, right_weight, right_bias, mask_float, marker)
    rows_left, rows_right = (
        lax.all_gather(left, "col", axis=1, tiled=True),
        lax.all_gather(right, "col", axis=1, tiled=True),
    )
    deep_left, deep_right = (
        lax.all_gather(rows_left, "seq", axis=0, tiled=True),
        lax.all_gather(rows_right, "seq", axis=0, tiled=True),
    )
    whole_right = lax.all_gather(deep_right, "row", axis=1, tiled=True)
    joint = outer_block(deep_left, column_block(whole_right))
    flat_sums, count_sums = split_joint(joint)
    return finish(flat_sums, count_sums, pair_state, pair_weight)


def solution(mesh):
    placed = (
        P("seq", ("row", "col"), None),
        P("seq", ("row", "col")),
        P(),
        P(),
        P(),
        P(),
        P(),
        P(),
        P(),
        P("row", "col", None),
    )
    return jax.shard_map(
        on_device, mesh=mesh, in_specs=placed, out_specs=P("row", "col", None), check_vma=False
    )
```

profile of v0, /device:TPU:0, one launch (start us, length us, event | category | flops | bytes accessed | tf_op | source)
XLA Modules:
  0.0 45.6 jit_solution(13767113097260525965)
XLA Ops:
  0.0 0.0 copy-start
  0.0 0.7 %fusion.19 = (f32[64,2]{0,1:T(2,128)S(1)}, bf16[64,2,1]{0,1,2:T(2,128)(2,1)S(1)}) fusion(s32[64,2]{0,1:T(2,128)} %param.11), kind=kLoop, calls=%fused_computation.32 | loop fusion | flops 256 | bytes 1280 | tf_op jit(solution)/shard_map/convert_element_type | solution.py:76
  0.8 1.0 %convert_reduce_fusion = f32[64,2]{1,0:T(8,128)S(1)} fusion(bf16[64,2,256]{2,1,0:T(2,128)(2,1)} %param.10), kind=kLoop, calls=%fused_computation.12 | loop fusion | flops 65408 | bytes 66048 | tf_op jit(solution)/shard_map/reduce_sum | solution.py:12
  1.8 1.1 %fusion.9 = f32[64,2]{1,0:T(8,128)S(1)} fusion(bf16[64,2,256]{2,1,0:T(2,128)(2,1)} %param.10, f32[64,2]{1,0:T(8,128)S(1)} %broadcast_multiply_fusion), kind=kLoop, calls=%fused_computation.15 | loop fusion | flops 130944 | bytes 66560 | tf_op jit(solution)/shard_map/reduce_sum | solution.py:13
  2.8 1.1 %fusion.12 = bf16[64,2,256]{2,1,0:T(2,128)(2,1)S(1)} fusion(bf16[64,2,256]{2,1,0:T(2,128)(2,1)} %param.10, f32[256]{0:T(256)} %param.13, f32[256]{0:T(256)} %param.12, f32[64,2]{1,0:T(8,128)S(1)} %add_rsqrt_fusion, f32[64,2]{1,0:T(8,128)S(1)} %broadcast_multiply_fusion), kind=kLoop, calls=%fused_computation.18 | loop fusion | flops 196608 | bytes 134144 | tf_op jit(solution)/shard_map/convert_element_type | solution.py:14
  3.9 0.8 %fusion.4 = bf16[64,2,32]{0,2,1:T(8,128)(2,1)S(1)} fusion(bf16[64,2,256]{2,1,0:T(2,128)(2,1)S(1)} %fusion.12, bf16[256,32]{0,1:T(8,128)(2,1)} %param.16, f32[32]{0:T(128)} %param.17, f32[64,2]{0,1:T(2,128)S(1)} %get-tuple-element.7), kind=kOutput, calls=%fused_computation.8 | convolution fusion | flops 2109440 | bytes 90752 | tf_op jit(solution)/shard_map/dot_general | solution.py:21
  4.8 0.9 %fusion.3 = bf16[64,2,32]{0,2,1:T(8,128)(2,1)S(1)} fusion(bf16[64,2,256]{2,1,0:T(2,128)(2,1)S(1)} %fusion.12, bf16[256,32]{0,1:T(8,128)(2,1)} %param.14, f32[64,2]{0,1:T(2,128)S(1)} %get-tuple-element.7, f32[32]{0:T(128)} %param.15), kind=kOutput, calls=%fused_computation.7 | convolution fusion | flops 2109440 | bytes 90752 | tf_op jit(solution)/shard_map/dot_general | solution.py:21
  5.7 0.1 pad_maximum_fusion.1
  5.7 9.8 %all_gather.15 = bf16[64,8,33]{0,2,1:T(8,128)(2,1)S(1)} all-gather(bf16[64,2,33]{0,2,1:T(8,128)(2,1)S(1)} %get-tuple-element.5), channel_id=1, replica_groups=mesh['seq'=2,'row'=4,'col'=4] {'col'}, dimensions={1}, use_global_device_ids=true | all-gather | bytes 42240 | tf_op jit(solution)/shard_map/all_gather | solution.py:81
  15.6 0.2 copy.21
  15.7 8.3 %all_gather.17 = bf16[64,8,33]{0,2,1:T(8,128)(2,1)S(1)} all-gather(bf16[64,2,33]{0,2,1:T(8,128)(2,1)S(1)} %get-tuple-element.6), channel_id=1, replica_groups=mesh['seq'=2,'row'=4,'col'=4] {'col'}, dimensions={1}, use_global_device_ids=true | all-gather | bytes 42240 | tf_op jit(solution)/shard_map/all_gather | solution.py:82
  24.0 0.2 copy.25
  24.2 2.0 %all_gather.18 = bf16[128,8,33]{2,1,0:T(8,128)(2,1)S(1)} all-gather(bf16[64,8,33]{2,1,0:T(8,128)(2,1)S(1)} %copy.25), channel_id=1, replica_groups=mesh['seq'=2,'row'=4,'col'=4] {'seq'}, dimensions={0}, use_global_device_ids=true | all-gather | bytes 101376 | tf_op jit(solution)/shard_map/all_gather | solution.py:86
  26.2 0.2 copy.26
  26.4 2.0 %all_gather.16 = bf16[128,8,33]{2,1,0:T(8,128)(2,1)S(1)} all-gather(bf16[64,8,33]{2,1,0:T(8,128)(2,1)S(1)} %copy.21), channel_id=1, replica_groups=mesh['seq'=2,'row'=4,'col'=4] {'seq'}, dimensions={0}, use_global_device_ids=true | all-gather | bytes 101376 | tf_op jit(solution)/shard_map/all_gather | solution.py:85
  28.4 0.2 reshape.44
  28.6 0.1 copy.29
  28.8 14.3 %all_gather.19 = bf16[128,32,33]{0,1,2:T(8,128)(2,1)S(1)} all-gather(bf16[128,8,33]{0,1,2:T(8,128)(2,1)S(1)} %copy.26), channel_id=1, replica_groups=mesh['seq'=2,'row'=4,'col'=4] {'row'}, dimensions={1}, use_global_device_ids=true | all-gather | bytes 337920 | tf_op jit(solution)/shard_map/all_gather | solution.py:88
  43.2 0.3 convolution_bitcast_fusion
  43.5 0.3 fusion.16
  43.8 0.0 copy-start.1
  43.8 0.1 slice.8
  43.9 0.5 %reshape.38 = f32[8,8,1024]{2,1,0:T(8,128)S(1)} reshape(f32[8,8,32,32]{3,2,1,0:T(8,128)S(1)} %slice.8) | data formatting | bytes 524288 | tf_op jit(solution)/shard_map/reshape | solution.py:41
  44.4 0.0 copy-done
  44.4 0.1 copy-done.1
  44.5 1.1 %fusion.5 = bf16[8,8,128]{2,1,0:T(8,128)(2,1)} fusion(f32[8,8,1024]{2,1,0:T(8,128)S(1)} %reshape.38, f32[1024,128]{1,0:T(8,128)S(1)} %copy-done, bf16[8,8,128]{2,1,0:T(8,128)(2,1)S(1)} %copy-done.1, f32[8,8]{1,0:T(8,128)S(1)} %fusion.16), kind=kOutput, calls=%fused_computation.9 | convolution fusion | flops 100696064 | bytes 819456 | tf_op jit(solution)/shard_map/dot_general | solution.py:50
  (8 shorter events, 0.2 us)
Async XLA Ops:
  0.0 44.4 %copy-start = (f32[1024,128]{1,0:T(8,128)S(1)}, f32[1024,128]{1,0:T(8,128)}, u32[]{:S(2)}) copy-start(f32[1024,128]{1,0:T(8,128)} %param.18) | copy-start | bytes 1572868
  43.8 0.7 %copy-start.1 = (bf16[8,8,128]{2,1,0:T(8,128)(2,1)S(1)}, bf16[8,8,128]{2,1,0:T(8,128)(2,1)}, u32[]{:S(2)}) copy-start(bf16[8,8,128]{2,1,0:T(8,128)(2,1)} %param.19) | copy-start | bytes 49156
where the time goes:
time: 46.1 us; the launch traced here: 45.6 us
  blocking collectives  36.4 us (79%)
  other arithmetic  4.18 us (9%)
  matrix products  3.14 us (7%)
  local copies, waits for them, and re-layouts  1.69 us (4%)
    all_gather x1, blocking collectives, on_device(): whole_right = lax.all_gather(deep_right, 'row', axis=1, tiled=True)  14.3 us
    all_gather x1, blocking collectives, on_device(): lax.all_gather(left, 'col', axis=1, tiled=True)  9.85 us
    all_gather x1, blocking collectives, on_device(): lax.all_gather(right, 'col', axis=1, tiled=True)  8.3 us
    all_gather x1, blocking collectives, on_device(): lax.all_gather(rows_right, 'seq', axis=0, tiled=True)  2 us
    all_gather x1, blocking collectives, on_device(): lax.all_gather(rows_left, 'seq', axis=0, tiled=True)  1.99 us
    dot_general x2, matrix products, project(): jnp.dot(normed, weight, preferred_element_type=jnp.float32) + offset  1.73 us
    reduce_sum x1, other arithmetic, layer_norm(): spread = jnp.mean((values - center) ** 2, axis=-1, keepdims=True)  1.06 us
    convert_element_type x1, other arithmetic, layer_norm(): ((values - center) * lax.rsqrt(spread + variance_floor) * norm_gain + nor...  1.06 us

commit v1 on v0

v1 whole, which is shorter than its diff:
```python
import functools

import jax
import jax.numpy as jnp
from jax import lax
from jax.experimental import pallas as pl
from jax.experimental.pallas import tpu as pltpu
from jax.sharding import PartitionSpec as P

variance_floor = 1e-05
count_floor = 0.001
LANES = 128
MESH = pl.DeviceIdType.MESH
NT = (((1,), (1,)), ((), ()))


def device(seq, row, col):
    return {"seq": seq, "row": row, "col": col}


def kernel(
    sizes,
    x_hbm, mask_hbm, gain_hbm, shift_hbm, wl_hbm, bl_hbm, wr_hbm, br_hbm, pw_hbm, pair_hbm,
    out_ref,
    x_v, xf_v, mask_v, gain_v, shift_v, w_v, bl_v, br_v, pw_v, pair_v, w2_v,
    lbuf, rbuf, rsend, mlbuf, mrbuf, msend, cbuf, pbuf, prod_v, flat_v,
    in_sem,
    l_send, l_recv, r_send, r_recv, ml_send, ml_recv, mr_send, mr_recv,
    c_send, c_recv, p_send, p_recv,
):
    nseq, nrow, ncol, S, nres, CM, CH = sizes
    nI, nJ = ncol * nres, nrow * nres
    G = LANES // CH
    s, r, c = lax.axis_index("seq"), lax.axis_index("row"), lax.axis_index("col")
    q = r * ncol + c
    target_col, slot = q // nrow, q % nrow
    is_self = target_col == c

    def right_source(t):
        owner = c * nrow + t
        return owner, device(s, owner // ncol, owner % ncol)

    barrier = pltpu.get_barrier_semaphore()
    for d in range(1, ncol):
        pl.semaphore_signal(
            barrier, inc=1, device_id=device(s, r, (c + ncol - d) % ncol), device_id_type=MESH
        )
    for t in range(nrow):
        owner, where = right_source(t)

        @pl.when(owner != q)
        def _():
            pl.semaphore_signal(barrier, inc=1, device_id=where, device_id_type=MESH)

    for d in range(1, nseq):
        pl.semaphore_signal(
            barrier, inc=1, device_id=device((s + nseq - d) % nseq, r, c), device_id_type=MESH
        )

    pairs = [
        (mask_hbm, mask_v),
        (x_hbm, x_v),
        (gain_hbm, gain_v),
        (shift_hbm, shift_v),
        (wl_hbm, w_v.at[pl.ds(0, CH)]),
        (wr_hbm, w_v.at[pl.ds(CH, CH)]),
        (bl_hbm, bl_v),
        (br_hbm, br_v),
        (pw_hbm, pw_v),
        (pair_hbm, pair_v),
    ]
    local = [pltpu.make_async_copy(a, b, in_sem.at[k]) for k, (a, b) in enumerate(pairs)]
    for copy in local:
        copy.start()

    def left_copy(d, src, dst, send, recv):
        return pltpu.make_async_remote_copy(
            src_ref=src, dst_ref=dst.at[c], send_sem=send.at[d], recv_sem=recv.at[c],
            device_id=device(s, r, (c + d) % ncol), device_id_type=MESH,
        )

    def right_copy(d, src, dst, send, recv):
        return pltpu.make_async_remote_copy(
            src_ref=src, dst_ref=dst.at[slot], send_sem=send.at[d], recv_sem=recv.at[slot],
            device_id=device(s, (r + d) % nrow, target_col), device_id_type=MESH,
        )

    def seq_copy(d, buf, send, recv):
        return pltpu.make_async_remote_copy(
            src_ref=buf.at[s], dst_ref=buf.at[s], send_sem=send.at[d], recv_sem=recv.at[s],
            device_id=device((s + d) % nseq, r, c), device_id_type=MESH,
        )

    def start_left(src, dst, send, recv):
        for d in reversed(range(1, ncol)):
            left_copy(d, src, dst, send, recv).start()

    def start_right(src, dst, send, recv):
        for d in reversed(range(1, nrow)):
            right_copy(d, src, dst, send, recv).start()

        @pl.when(jnp.logical_not(is_self))
        def _():
            right_copy(0, src, dst, send, recv).start()

    def arrive_left(dst, send, recv):
        for d in range(1, ncol):
            peer = (c + d) % ncol
            pltpu.make_async_remote_copy(
                src_ref=dst.at[peer], dst_ref=dst.at[peer], send_sem=send.at[d],
                recv_sem=recv.at[peer], device_id=device(s, r, peer), device_id_type=MESH,
            ).wait_recv()

    def arrive_right(dst, send, recv):
        for t in range(nrow):
            owner, where = right_source(t)

            @pl.when(owner != q)
            def _():
                pltpu.make_async_remote_copy(
                    src_ref=dst.at[t], dst_ref=dst.at[t], send_sem=send.at[0],
                    recv_sem=recv.at[t], device_id=where, device_id_type=MESH,
                ).wait_recv()

    def arrive_seq(buf, send, recv):
        for d in range(1, nseq):
            peer = (s + d) % nseq
            pltpu.make_async_remote_copy(
                src_ref=buf.at[peer], dst_ref=buf.at[peer], send_sem=send.at[d],
                recv_sem=recv.at[peer], device_id=device(peer, r, c), device_id_type=MESH,
            ).wait_recv()

    local[0].wait()
    mask_row = jnp.concatenate(
        [mask_v[k : k + 1, :].astype(jnp.float32) for k in range(nres)], axis=1
    )
    mask_block = jnp.broadcast_to(mask_row, (8, nres * S))
    mlbuf[c] = mask_block
    msend[...] = mask_block

    @pl.when(is_self)
    def _():
        mrbuf[slot] = mask_block

    pl.semaphore_wait(barrier, ncol - 1 + nseq - 1 + nrow - is_self.astype(jnp.int32))
    start_left(msend, mlbuf, ml_send, ml_recv)
    start_right(msend, mrbuf, mr_send, mr_recv)

    for copy in local[1:8]:
        copy.wait()
    H = CM // LANES
    xf_v[...] = x_v[...].astype(jnp.float32)
    halves = [
        jnp.concatenate(
            [xf_v[pl.ds(h * nres + k, S, stride=H * nres), :] for k in range(nres)], axis=0
        )
        for h in range(H)
    ]
    center = sum(jnp.sum(v, axis=-1, keepdims=True) for v in halves) * (1.0 / CM)
    halves = [v - center for v in halves]
    spread = sum(jnp.sum(v * v, axis=-1, keepdims=True) for v in halves) * (1.0 / CM)
    scale = lax.rsqrt(spread + variance_floor)
    normed = jnp.concatenate(
        [
            (
                v * scale * gain_v[:, h * LANES : (h + 1) * LANES]
                + shift_v[:, h * LANES : (h + 1) * LANES]
            ).astype(jnp.bfloat16)
            for h, v in enumerate(halves)
        ],
        axis=1,
    )
    offsets = jnp.concatenate(
        [bl_v[...], br_v[...], jnp.zeros((1, LANES - 2 * CH), jnp.float32)], axis=1
    )
    offset_column = jnp.broadcast_to(offsets, (LANES, LANES)).T[: 2 * CH, :]
    both = lax.dot_general(w_v[...], normed, NT, preferred_element_type=jnp.float32)
    both = ((both + offset_column) * mask_row).astype(jnp.bfloat16)
    rsend[...] = both[CH:, :]
    lbuf[c] = both[:CH, :]

    @pl.when(is_self)
    def _():
        rbuf[slot] = both[CH:, :]

    start_right(rsend, rbuf, r_send, r_recv)
    start_left(lbuf.at[c], lbuf, l_send, l_recv)

    local[8].wait()
    local[9].wait()
    weight = pw_v[...]
    high = weight.astype(jnp.bfloat16)
    w2_v[:, :LANES] = high
    w2_v[:, LANES:] = (weight - high.astype(jnp.float32)).astype(jnp.bfloat16)

    def stack(buf, count, rows):
        return jnp.concatenate(
            [buf[d, :rows, k * S : (k + 1) * S] for d in range(count) for k in range(nres)], axis=0
        )

    arrive_left(mlbuf, ml_send, ml_recv)
    arrive_right(mrbuf, mr_send, mr_recv)
    row_masks = jnp.concatenate(
        [stack(mlbuf, ncol, 1), jnp.zeros((LANES - nI, S), jnp.float32)], axis=0
    )
    cbuf[s] = lax.dot_general(
        stack(mrbuf, nrow, 1).astype(jnp.bfloat16),
        row_masks.astype(jnp.bfloat16),
        NT,
        preferred_element_type=jnp.float32,
    )
    for d in range(1, nseq):
        seq_copy(d, cbuf, c_send, c_recv).start()

    arrive_left(lbuf, l_send, l_recv)
    arrive_right(rbuf, r_send, r_recv)
    product = lax.dot_general(
        stack(lbuf, ncol, CH), stack(rbuf, nrow, CH), NT, preferred_element_type=jnp.float32
    )
    for t in range(nJ // G):
        prod_v[t] = product[:, t * LANES : (t + 1) * LANES]
    for group in range(nI // 8):
        for g in range(CH // G):
            for t in range(nJ // G):
                rows = [
                    prod_v[t, pl.ds(group * 8 * CH + g * G + k, 8, stride=CH), :] for k in range(G)
                ]
                for j in range(G):
                    base = (group * nJ + t * G + j) * 8
                    flat_v[base : base + 8, g * LANES : (g + 1) * LANES] = jnp.concatenate(
                        [v[:, j * CH : (j + 1) * CH] for v in rows], axis=1
                    )
    flat = flat_v[...]
    flat_high = flat.astype(jnp.bfloat16)
    flat_low = (flat - flat_high.astype(jnp.float32)).astype(jnp.bfloat16)
    wide = jnp.dot(flat_high, w2_v[...], preferred_element_type=jnp.float32)
    narrow = jnp.dot(flat_low, w2_v[:, :LANES], preferred_element_type=jnp.float32)
    pbuf[s] = wide[:, :LANES] + (wide[:, LANES:] + narrow)
    for d in range(1, nseq):
        seq_copy(d, pbuf, p_send, p_recv).start()

    arrive_seq(cbuf, c_send, c_recv)
    inverse = 1.0 / (count_floor + sum(cbuf[k] for k in range(nseq)))
    arrive_seq(pbuf, p_send, p_recv)
    for i in range(nI):
        start = (i // 8) * nJ * 8 + i % 8
        total = sum(pbuf[k, pl.ds(start, nJ, stride=8), :] for k in range(nseq))
        out_ref[i] = (
            pair_v[i].astype(jnp.float32) + total * inverse[:, i : i + 1]
        ).astype(jnp.bfloat16)

    for d in range(1, ncol):
        left_copy(d, msend, mlbuf, ml_send, ml_recv).wait_send()
        left_copy(d, lbuf.at[c], lbuf, l_send, l_recv).wait_send()
    for d in range(1, nrow):
        right_copy(d, msend, mrbuf, mr_send, mr_recv).wait_send()
        right_copy(d, rsend, rbuf, r_send, r_recv).wait_send()

    @pl.when(jnp.logical_not(is_self))
    def _():
        right_copy(0, msend, mrbuf, mr_send, mr_recv).wait_send()
        right_copy(0, rsend, rbuf, r_send, r_recv).wait_send()

    for d in range(1, nseq):
        seq_copy(d, cbuf, c_send, c_recv).wait_send()
        seq_copy(d, pbuf, p_send, p_recv).wait_send()


def on_device(
    nseq, nrow, ncol,
    alignment, row_mask, norm_gain, norm_bias, left_weight, left_bias,
    right_weight, right_bias, pair_weight, pair_state,
):
    S, nres, CM = alignment.shape
    CH = left_weight.shape[1]
    CZ = pair_weight.shape[1]
    H = CM // LANES
    nI, nJ = ncol * nres, nrow * nres
    f32, bf16 = jnp.float32, jnp.bfloat16
    view = (
        alignment.reshape(S, nres, H, LANES).transpose(0, 2, 1, 3).reshape(S * H * nres, LANES)
    )
    dma = pltpu.SemaphoreType.DMA
    return pl.pallas_call(
        functools.partial(kernel, (nseq, nrow, ncol, S, nres, CM, CH)),
        out_shape=jax.ShapeDtypeStruct(pair_state.shape, bf16),
        in_specs=[pl.BlockSpec(memory_space=pl.ANY)] * 10,
        out_specs=pl.BlockSpec(memory_space=pltpu.VMEM),
        scratch_shapes=[
            pltpu.VMEM((S * H * nres, LANES), bf16),
            pltpu.VMEM((S * H * nres, LANES), f32),
            pltpu.VMEM((nres, S), jnp.int32),
            pltpu.VMEM((1, CM), f32),
            pltpu.VMEM((1, CM), f32),
            pltpu.VMEM((2 * CH, CM), bf16),
            pltpu.VMEM((1, CH), f32),
            pltpu.VMEM((1, CH), f32),
            pltpu.VMEM(pair_weight.shape, f32),
            pltpu.VMEM(pair_state.shape, bf16),
            pltpu.VMEM((CH * CH, 2 * CZ), bf16),
            pltpu.VMEM((ncol, CH, nres * S), bf16),
            pltpu.VMEM((nrow, CH, nres * S), bf16),
            pltpu.VMEM((CH, nres * S), bf16),
            pltpu.VMEM((ncol, 8, nres * S), f32),
            pltpu.VMEM((nrow, 8, nres * S), f32),
            pltpu.VMEM((8, nres * S), f32),
            pltpu.VMEM((nseq, nJ, LANES), f32),
            pltpu.VMEM((nseq, nI * nJ, CZ), f32),
            pltpu.VMEM((nJ * CH // LANES, nI * CH, LANES), f32),
            pltpu.VMEM((nI * nJ, CH * CH), f32),
            dma((10,)),
            dma((ncol,)), dma((ncol,)), dma((nrow,)), dma((nrow,)),
            dma((ncol,)), dma((ncol,)), dma((nrow,)), dma((nrow,)),
            dma((nseq,)), dma((nseq,)), dma((nseq,)), dma((nseq,)),
        ],
        compiler_params=pltpu.CompilerParams(collective_id=0, has_side_effects=True),
    )(
        view,
        row_mask.T,
        norm_gain.reshape(1, CM),
        norm_bias.reshape(1, CM),
        left_weight.T,
        left_bias.reshape(1, CH),
        right_weight.T,
        right_bias.reshape(1, CH),
        pair_weight,
        pair_state,
    )


def solution(mesh):
    placed = (
        P("seq", ("row", "col"), None),
        P("seq", ("row", "col")),
        P(), P(), P(), P(), P(), P(), P(),
        P("row", "col", None),
    )
    return jax.shard_map(
        functools.partial(
            on_device, mesh.shape["seq"], mesh.shape["row"], mesh.shape["col"]
        ),
        mesh=mesh, in_specs=placed, out_specs=P("row", "col", None), check_vma=False,
    )
```

time: 46.1 us -> 13.9 us (0.30)
  blocking collectives: 36.4 us -> 0 us
  Pallas kernels: 0 us -> 12.3 us
  other arithmetic: 4.18 us -> 0 us
  matrix products: 3.14 us -> 0 us
    all_gather x5 -> x0, blocking collectives: 36.4 us -> none  [the longest x1 14.3 us: on_device(): whole_right = lax.all_gather(deep_right, 'row', axis=1, tiled=True)]
    pallas_call x0 -> x1, Pallas kernels: none -> 12.3 us  [on_device(): pl.pallas_call(functools.partial(kernel, (nseq, nrow, ncol, S, nres, CM,...]
    dot_general x4 -> x0, matrix products: 3.14 us -> none  [the longest x2 1.73 us: project(): jnp.dot(normed, weight, preferred_element_type=jnp.float32) + offset]
    reduce_sum x2 -> x0, other arithmetic: 2.04 us -> none  [the longest x1 1.06 us: layer_norm(): spread = jnp.mean((values - center) ** 2, axis=-1, keepdims=True)]
    convert_element_type x2 -> x0, other arithmetic: 1.8 us -> none  [the longest x1 1.06 us: layer_norm(): ((values - center) * lax.rsqrt(spread + variance_floor) * norm_gain + nor...]
    unnamed x4 -> x1, local copies, waits for them, and re-layouts: 0.09 us -> 1.32 us
    reshape x4 -> x0, local copies, waits for them, and re-layouts: 0.84 us -> none  [the longest x1 0.49 us: split_joint(): joint[:, :, :channels, :channels]]
    all_gather x3 -> x0, local copies, waits for them, and re-layouts: 0.54 us -> none  [the longest x1 0.22 us: on_device(): lax.all_gather(rows_right, 'seq', axis=0, tiled=True)]
where the time goes in v1:
time: 13.9 us; the launch traced here: 13.7 us
  Pallas kernels  12.3 us (88%)
  local copies, waits for them, and re-layouts  1.32 us (9%)
    pallas_call x1, Pallas kernels, on_device(): pl.pallas_call(functools.partial(kernel, (nseq, nrow, ncol, S, nres, CM,...  12.3 us
    unnamed x1, local copies, waits for them, and re-layouts  1.32 us

profile of v1, /device:TPU:0, one launch (start us, length us, event | category | flops | bytes accessed | tf_op | source)
XLA Modules:
  0.0 13.7 jit_solution(9546145220154257146)
XLA Ops:
  0.0 12.3 %shard_map.100 = bf16[8,8,128]{2,1,0:T(8,128)(2,1)} custom-call(bf16[256,128]{1,0:T(8,128)(2,1)} %bitcast.12, s32[2,64]{1,0:T(2,128)} %bitcast.15, f32[1,256]{1,0:T(1,128)} %bitcast.16, f32[1,256]{1,0:T(1,128)} %bitcast.17, bf16[32,256]{1,0:T(8,128)(2,1)} %bitcast.13, f32[1,32]{1,0:T(1,128)} %bitcast.18, bf16[32,256]{1,0:T(8,128)(2,1)} %bitcast.14, ...), custom_call_target="tpu_custom_call" | custom-call | tf_op jit(solution)/shard_map/pallas_call | solution.py:284
  12.3 1.3 %copy.13 = bf16[8,8,128]{2,1,0:T(8,128)(2,1)} copy(bf16[8,8,128]{2,1,0:T(8,128)(2,1)} %shard_map.100) | data formatting | bytes 32768
